TPU v7x, 512 devices: a 8x2x16 block of a 8x8x16 slice. The times are simulated.
512 devices in a mesh: groups: 2 (over y), prompt: 16 (over z), sample: 8 (over x), head: 2 (over core).
Axes of the slice: x: 8, y: 2, z: 16, core: 2. Of those that a mesh axis runs over, the one named last changes fastest.
The devices are a block of a 8x8x16 slice.
Arguments:
- queries: bfloat16 [1024, 16, 576], P(('groups', 'prompt', 'sample'), 'head'), parts along dimension 0, may hold values from -6 to 6
- prompt_cache: bfloat16 [64, 1024, 576], P(('groups', 'prompt'), 'sample'), parts along dimension 0, may hold values from -6 to 6
- suffix_cache: bfloat16 [1024, 64, 576], P(('groups', 'prompt', 'sample')), parts along dimension 0, may hold values from -6 to 6
- suffix_len: int32 [1024], P(('groups', 'prompt', 'sample')), parts along dimension 0, may hold values from 2 to 64, as said below
- sample_prompt: int32 [1024], P('groups'), parts along dimension 0, may hold values from 0 to 31, as said below
- prompt_slot: int32 [64], P('groups'), parts along dimension 0, may hold values from 0 to 31, as said below
Outputs:
- attended: bfloat16 [1024, 16, 512], P(('groups', 'prompt', 'sample'), 'head'), parts along dimension 0
There are 2 independent parts, one for each index of `groups`. A program takes and returns all parts, laid end to end along the dimension named above; each array names one. Nothing has to cross between parts.
Inputs may be any that keep to these rules, and one draw needn't show every extreme that they name: `suffix_len`: the value 64 is reached. Every prompt is named by exactly 16 samples; in each aligned block of 4 samples, prompt_slot[sample_prompt] // 2 takes no value more than 1 times, and some value exactly 1 times. `prompt_slot`: a permutation.
All inputs are finite; a program needn't handle non-finite values.
Results may differ from a plain program's by a relative error of at most 0.013.
Values may be sent and summed in bfloat16 or wider, within the bound.
A program may use at most 64 MiB of HBM per device.

v0:
```python
import math

import jax
import jax.numpy as jnp
from jax import lax
from jax.sharding import PartitionSpec as P

DL = 512
DR = 64
QKN = 128
SPP = 16
P_DEV = 2


def side_by_side(arrays, axis, split_dim, concat_dim, along):
    widths = [math.prod(a.shape[along:]) for a in arrays]
    both = jnp.concatenate(
        [a.reshape(*a.shape[:along], w) for a, w in zip(arrays, widths)], axis=along
    )
    filled = lax.all_to_all(both, axis, split_axis=split_dim, concat_axis=concat_dim, tiled=True)
    tiles = jnp.split(filled, [sum(widths[:k]) for k in range(1, len(widths))], axis=along)
    return tuple(
        (b.reshape(*filled.shape[:along], *a.shape[along:]) for a, b in zip(arrays, tiles))
    )


def partial_softmax(asked, keys, score_form, value_form, scaling, allowed):
    scores = jnp.einsum(score_form, asked, keys, preferred_element_type=jnp.float32) * scaling
    if allowed is not None:
        scores = jnp.where(allowed, scores, -1e30)
    row_max = jnp.max(scores, axis=-1)
    weights = jnp.exp(scores - row_max[..., None])
    row_sum = jnp.sum(weights, axis=-1)
    row_out = jnp.einsum(
        value_form, weights.astype(jnp.bfloat16), keys[..., :DL], preferred_element_type=jnp.float32
    )
    return (row_max, row_sum, row_out)


def routing_tables(sample_prompt, prompt_slot, device_count, per_device, owner_count, send_count):
    slot_index = jnp.take(prompt_slot, sample_prompt)
    owner_of = (slot_index // P_DEV).reshape(device_count, per_device)
    local_prompt = slot_index % P_DEV
    owners = jnp.arange(owner_count, dtype=jnp.int32)
    owner_hot = (owner_of[:, :, None] == owners[None, None, :]).astype(jnp.int32)
    rank_in = jnp.sum((jnp.cumsum(owner_hot, axis=1) - 1) * owner_hot, axis=2)
    places = jnp.arange(send_count, dtype=jnp.int32)
    matches = (owner_of[:, :, None, None] == owners[None, None, :, None]) & (
        rank_in[:, :, None, None] == places[None, None, None, :]
    )
    counter = jnp.arange(per_device, dtype=jnp.int32)[None, :, None, None]
    positions = jnp.sum(matches.astype(jnp.int32) * counter, axis=1)
    present = jnp.any(matches, axis=1)
    return (owner_of, rank_in, positions, present, local_prompt)


def prefix_partials(rows, row_samples, row_valid, local_prompt, prompt_cache, head_count, scaling):
    row_count = rows.shape[0]
    group_count = P_DEV * SPP
    feature_count = prompt_cache.shape[2]
    row_prompt = jnp.take(local_prompt, row_samples)
    prompt_hot = (
        (row_prompt[:, None] == jnp.arange(P_DEV, dtype=jnp.int32)[None, :]) & row_valid[:, None]
    ).astype(jnp.int32)
    prompt_rank = jnp.sum((jnp.cumsum(prompt_hot, axis=0) - 1) * prompt_hot, axis=1)
    grouped_at = row_prompt * SPP + prompt_rank
    marked = jnp.where(row_valid, grouped_at, -1)
    fetch_at = jnp.where(row_valid, grouped_at, 0)
    counter = jnp.arange(row_count, dtype=jnp.int32)
    places = jnp.arange(group_count, dtype=jnp.int32)
    source_row = jnp.sum(
        (marked[None, :] == places[:, None]).astype(jnp.int32) * counter[None, :], axis=1
    )
    grouped = jnp.take(rows, source_row, axis=0).reshape(P_DEV, SPP, head_count, feature_count)
    row_max, row_sum, row_out = partial_softmax(
        grouped, prompt_cache, "kshf,ktf->ksht", "ksht,ktd->kshd", scaling, None
    )
    row_max = jnp.take(row_max.reshape(group_count, head_count), fetch_at, axis=0)
    row_sum = jnp.take(row_sum.reshape(group_count, head_count), fetch_at, axis=0)
    row_out = jnp.take(row_out.reshape(group_count, head_count, DL), fetch_at, axis=0)
    return (row_max, row_sum, row_out)


def body(queries, prompt_cache, suffix_cache, suffix_len, sample_prompt, prompt_slot):
    per_device, head_count, feature_count = queries.shape
    owner_count = lax.axis_size("prompt")
    slice_count = lax.axis_size("sample")
    device_count = owner_count * slice_count
    send_count = max(1, per_device // owner_count)
    row_width = head_count * feature_count
    scaling = 1.0 / math.sqrt(QKN + DR)
    owner_of, rank_in, positions, present, local_prompt = routing_tables(
        sample_prompt, prompt_slot, device_count, per_device, owner_count, send_count
    )
    device = lax.axis_index(("prompt", "sample"))
    owner_index = lax.axis_index("prompt")
    flat_queries = queries.reshape(per_device, row_width)
    send_rows = lax.dynamic_index_in_dim(positions, device, 0, keepdims=False).reshape(-1)
    outgoing = jnp.take(flat_queries, send_rows, axis=0).reshape(owner_count, send_count, row_width)
    arrive_pos = lax.dynamic_index_in_dim(positions, owner_index, 1, keepdims=False)
    arrive_valid = lax.dynamic_index_in_dim(present, owner_index, 1, keepdims=False)
    arrive_ids = jnp.arange(device_count, dtype=jnp.int32)[:, None] * per_device + arrive_pos
    fanned = jnp.broadcast_to(outgoing[:, None], (owner_count, slice_count, send_count, row_width))
    fanned = fanned.reshape(device_count * send_count, row_width)
    arrived = lax.all_to_all(fanned, ("prompt", "sample"), split_axis=0, concat_axis=0, tiled=True)
    partials = prefix_partials(
        arrived,
        arrive_ids.reshape(-1),
        arrive_valid.reshape(-1),
        local_prompt,
        prompt_cache,
        head_count,
        scaling,
    )
    back_max, back_sum, back_out = side_by_side(
        (partials[0], partials[1], partials[2]), ("prompt", "sample"), 0, 0, 2
    )
    back_max = back_max.reshape(owner_count, slice_count, send_count, head_count)
    back_sum = back_sum.reshape(owner_count, slice_count, send_count, head_count)
    back_out = back_out.reshape(owner_count, slice_count, send_count, head_count, DL)
    prefix_max = jnp.max(back_max, axis=1)
    rescale = jnp.exp(back_max - prefix_max[:, None])
    prefix_sum = jnp.sum(back_sum * rescale, axis=1)
    prefix_out = jnp.sum(back_out * rescale[..., None], axis=1)
    prefix_max = prefix_max.reshape(owner_count * send_count, head_count)
    prefix_sum = prefix_sum.reshape(owner_count * send_count, head_count)
    prefix_out = prefix_out.reshape(owner_count * send_count, head_count, DL)
    own_owner = lax.dynamic_index_in_dim(owner_of, device, 0, keepdims=False)
    own_rank = lax.dynamic_index_in_dim(rank_in, device, 0, keepdims=False)
    own_at = own_owner * send_count + own_rank
    pre_max = jnp.take(prefix_max, own_at, axis=0)
    pre_sum = jnp.take(prefix_sum, own_at, axis=0)
    pre_out = jnp.take(prefix_out, own_at, axis=0)
    suffix_tokens = suffix_cache.shape[1]
    allowed = (jnp.arange(suffix_tokens, dtype=jnp.int32)[None, :] < suffix_len[:, None])[
        :, None, :
    ]
    suf_max, suf_sum, suf_out = partial_softmax(
        queries, suffix_cache, "shf,stf->sht", "sht,std->shd", scaling, allowed
    )
    both_max = jnp.maximum(pre_max, suf_max)
    weight_pre = jnp.exp(pre_max - both_max)
    weight_suf = jnp.exp(suf_max - both_max)
    numerator = weight_pre[..., None] * pre_out + weight_suf[..., None] * suf_out
    denominator = weight_pre * pre_sum + weight_suf * suf_sum
    return (numerator / denominator[..., None]).astype(jnp.bfloat16)


def solution(mesh):
    return jax.shard_map(
        body,
        mesh=mesh,
        in_specs=(
            P(("groups", "prompt", "sample"), "head", None),
            P(("groups", "prompt"), "sample", None),
            P(("groups", "prompt", "sample"), None, None),
            P(("groups", "prompt", "sample")),
            P("groups"),
            P("groups"),
        ),
        out_specs=P(("groups", "prompt", "sample"), "head", None),
        check_vma=False,
    )
```

profile of v0, /device:TPU:65, one launch (start us, length us, event | category | flops | bytes accessed | tf_op | source)
XLA Modules:
  0.0 296.9 jit_solution(4912961406098977968)
XLA Ops:
  0.0 2.1 fusion.44
  2.1 1.8 fusion.45
  3.9 20.8 %add_select_fusion = (s32[512]{0:T(512)S(1)}, s32[512]{0:T(512)S(1)}) fusion(s32[]{:T(128)} %bitcast.31, s32[]{:T(128)} %bitcast.30, s32[]{:T(128)} %bitcast.29, s32[]{:T(128)} %bitcast.28, s32[]{:T(128)} %bitcast.27, s32[]{:T(128)} %bitcast.26, s32[]{:T(128)} %bitcast.25, s32[]{:T(128)} %bitcast.24, s32[]{:T(128)} %bitcast.23, s32[]{:T(128)} %bitcast.22, ...), kind=kLoop, calls=%fused_computation.67 | loop fusion | flops 40960 | bytes 6272 | tf_op jit(solution)/shard_map/jit(remainder)/select_n | solution.py:43
  25.2 0.9 reshape.422
  26.1 0.6 gather_fusion.1
  26.9 0.5 broadcast.678
  27.4 1.5 reduce.11
  28.9 1.2 reshape.565
  30.2 55.2 %all-to-all-start = ((bf16[128,2,2304]{2,1,0:T(2,128)(2,1)}), bf16[128,2,2304]{2,1,0:T(2,128)(2,1)}, u32[]{:S(2)}, u32[]{:S(2)}) async-start(bf16[128,2,2304]{2,1,0:T(2,128)(2,1)} %reshape.565), calls=%async_computation | async-start | bytes 2359296 | tf_op jit(solution)/shard_map/all_to_all | solution.py:105
  85.4 1.3 gather_fusion
  87.2 0.5 compare_and_fusion.1
  87.9 0.6 pad_clamp_fusion.4
  88.6 0.5 compare_and_fusion.3
  89.1 49.8 %all-to-all-done = bf16[128,2,2304]{2,1,0:T(2,128)(2,1)} async-done(((bf16[128,2,2304]{2,1,0:T(2,128)(2,1)}), bf16[128,2,2304]{2,1,0:T(2,128)(2,1)}, u32[]{:S(2)}, u32[]{:S(2)}) %all-to-all-start) | async-done | bytes 1179680 | tf_op jit(solution)/shard_map/all_to_all | solution.py:105
  138.9 6.8 %reshape.566 = bf16[128,1,4608]{2,1,0:T(2,128)(2,1)S(1)} reshape(bf16[128,2,2304]{2,1,0:T(2,128)(2,1)} %all-to-all-done) | data formatting | bytes 2359296
  145.9 1.0 gather_fusion.2
  146.9 0.3 gather.39
  147.2 0.4 fusion.47
  147.6 0.2 fusion.14
  147.8 0.3 fusion.8
  148.0 0.6 gather_fusion.6
  148.7 0.6 gather_fusion.5
  149.4 0.8 copy.63
  150.2 1.6 copy.64
  151.8 0.8 gather_fusion.3
  152.7 0.2 broadcast_select_fusion
  152.9 0.8 copy-done
  153.7 2.5 pad_maximum_fusion
  156.2 16.3 %all-to-all-start.1 = ((f32[128,8,514]{2,1,0:T(8,128)}), f32[128,8,514]{2,1,0:T(8,128)S(1)}, u32[]{:S(2)}, u32[]{:S(2)}) async-start(f32[128,8,514]{2,1,0:T(8,128)} %pad_maximum_fusion), calls=%async_computation.1 | async-start | bytes 5242880 | tf_op jit(solution)/shard_map/all_to_all | solution.py:20
  172.7 0.6 pad_clamp_fusion.1
  173.3 0.6 pad_clamp_fusion
  174.0 0.3 fusion.48
  174.2 0.8 fusion.23
  175.0 0.6 compare_and_fusion
  175.6 111.2 %all-to-all-done.1 = f32[128,8,514]{2,1,0:T(8,128)S(1)} async-done(((f32[128,8,514]{2,1,0:T(8,128)}), f32[128,8,514]{2,1,0:T(8,128)S(1)}, u32[]{:S(2)}, u32[]{:S(2)}) %all-to-all-start.1) | async-done | bytes 2105376 | tf_op jit(solution)/shard_map/all_to_all | solution.py:20
  286.8 0.9 fusion.43
  287.7 1.2 copy.65
  289.1 0.7 reshape_reshape.10
  289.9 0.7 subtract_exponential_fusion.1
  290.6 0.2 copy.68
  291.0 1.0 multiply_reduce_fusion.1
  292.1 0.7 gather_fusion.8
  292.7 0.7 gather_fusion.7
  293.4 0.9 copy.67
  294.3 0.6 split.13
  295.0 0.3 multiply_reduce_fusion
  295.3 0.7 gather_fusion.4
  296.0 0.8 fusion.2
  (60 shorter events, 2.5 us)
Async XLA Ops:
  30.2 108.8 %all-to-all-start = ((bf16[128,2,2304]{2,1,0:T(2,128)(2,1)}), bf16[128,2,2304]{2,1,0:T(2,128)(2,1)}, u32[]{:S(2)}, u32[]{:S(2)}) async-start(bf16[128,2,2304]{2,1,0:T(2,128)(2,1)} %reshape.565), calls=%async_computation | async-start | bytes 2359296 | tf_op jit(solution)/shard_map/all_to_all | solution.py:105
  145.9 1.3 copy-start.2
  145.9 1.3 copy-start.10
  146.9 2.5 copy-start.7
  152.6 1.0 copy-start
  156.2 17.7 %copy-start.9 = (s32[4]{0:T(128)S(1)}, s32[4]{0:T(128)}, u32[]{:S(2)}) copy-start(s32[4]{0:T(128)} %param.13) | copy-start | bytes 52
  156.2 17.7 %copy-start.1 = (bf16[4,64,576]{2,1,0:T(8,128)(2,1)S(1)}, bf16[4,64,576]{2,1,0:T(8,128)(2,1)}, u32[]{:S(2)}) copy-start(bf16[4,64,576]{2,1,0:T(8,128)(2,1)} %param.12) | copy-start | bytes 884740
  156.2 17.7 %copy-start.3 = (bf16[4,8,576]{2,1,0:T(8,128)(2,1)S(1)}, bf16[4,8,576]{2,1,0:T(8,128)(2,1)}, u32[]{:S(2)}) copy-start(bf16[4,8,576]{2,1,0:T(8,128)(2,1)} %param.10) | copy-start | bytes 110596
  156.2 130.6 %all-to-all-start.1 = ((f32[128,8,514]{2,1,0:T(8,128)}), f32[128,8,514]{2,1,0:T(8,128)S(1)}, u32[]{:S(2)}, u32[]{:S(2)}) async-start(f32[128,8,514]{2,1,0:T(8,128)} %pad_maximum_fusion), calls=%async_computation.1 | async-start | bytes 5242880 | tf_op jit(solution)/shard_map/all_to_all | solution.py:20
  174.2 0.8 copy-start.4
  295.0 1.0 copy-start.6
  295.0 1.0 copy-start.8
  295.0 1.1 copy-start.5
where the time goes:
time: 302 us; the launch traced here: 297 us
  waiting for transfers between devices  161 us (53%)
  starting transfers between devices  71.5 us (24%)
  other arithmetic  32.8 us (11%)
  local copies, waits for them, and re-layouts  29.5 us (10%)
    all_to_all x1, waiting for transfers between devices, side_by_side(): lax.all_to_all(both, axis, split_axis=split_dim, concat_axis=concat_dim,...  111 us
    all_to_all x1, starting transfers between devices, body(): lax.all_to_all(fanned, ('prompt', 'sample'), split_axis=0, concat_axis=0,...  55.2 us
    all_to_all x1, waiting for transfers between devices, body(): lax.all_to_all(fanned, ('prompt', 'sample'), split_axis=0, concat_axis=0,...  49.8 us
    select_n x1, other arithmetic, routing_tables(): local_prompt = slot_index % P_DEV  20.8 us
    all_to_all x1, starting transfers between devices, side_by_side(): lax.all_to_all(both, axis, split_axis=split_dim, concat_axis=concat_dim,...  16.3 us
    unnamed x25, local copies, waits for them, and re-layouts  8.99 us
  transfers between devices with their start and end apart: 2, of which 2 were waited for; matrix products, arithmetic and copies ran while one was open for 2% of the time, Pallas kernels for 0%

commit v1 on v0

v1 whole, which is shorter than its diff:
```python
import functools
import math

import jax
import jax.numpy as jnp
from jax import lax
from jax.experimental import pallas as pl
from jax.experimental.pallas import tpu as pltpu
from jax.sharding import PartitionSpec as P

DL = 512
DR = 64
QKN = 128
P_DEV = 2
MESH = pl.DeviceIdType.MESH
NT = (((1,), (1,)), ((), ()))
F32 = jnp.float32
BF16 = jnp.bfloat16


def far_first(n):
    return sorted(range(1, n), key=lambda r: -min(r, n - r))


def kernel(
    n_own,
    n_slice,
    sp_ref,
    ps_ref,
    sl_ref,
    q_hbm,
    cache_hbm,
    suffix_hbm,
    out_ref,
    q_vm,
    keys,
    suf_vm,
    stage,
    arrived,
    asked,
    acc,
    top,
    tot,
    res,
    stat,
    ret,
    ret_stat,
    suf_out,
    suf_top,
    suf_tot,
    local_sem,
    ring_send,
    ring_recv,
    pair_send,
    pair_recv,
    q_send,
    q_recv,
    r_send,
    r_recv,
    s_send,
    s_recv,
):
    per_dev, heads, feat = q_vm.shape
    tok = cache_hbm.shape[2]
    half = feat // 2
    rows = n_own * heads
    scaling = 1.0 / math.sqrt(QKN + DR)
    z = lax.axis_index("prompt")
    x = lax.axis_index("sample")
    h = lax.axis_index("head")
    right = lax.rem(x + 1, n_slice)
    left = lax.rem(x + n_slice - 1, n_slice)
    partner = 1 - h

    load_q = pltpu.make_async_copy(q_hbm, q_vm, local_sem.at[0])
    load_cache = pltpu.make_async_copy(cache_hbm, keys.at[:, 0], local_sem.at[1])
    load_suffix = pltpu.make_async_copy(suffix_hbm, suf_vm, local_sem.at[2])
    load_q.start()
    load_cache.start()
    load_suffix.start()

    barrier = pltpu.get_barrier_semaphore()
    for r in far_first(n_own):
        pl.semaphore_signal(
            barrier, inc=1, device_id={"prompt": lax.rem(z + r, n_own)}, device_id_type=MESH
        )
    pl.semaphore_signal(barrier, inc=1, device_id={"sample": right}, device_id_type=MESH)
    pl.semaphore_signal(barrier, inc=1, device_id={"sample": left}, device_id_type=MESH)
    pl.semaphore_signal(barrier, inc=1, device_id={"head": partner}, device_id_type=MESH)

    own = (z * n_slice + x) * per_dev
    places = []
    for j in range(per_dev):
        slot = ps_ref[sp_ref[own + j]]
        places.append(lax.rem((slot >> 1) - z + n_own, n_own))

    load_q.wait()
    for r in range(n_own):
        pick = jnp.int32(0)
        for j in range(1, per_dev):
            pick = jnp.where(places[j] == r, j, pick)
        row = q_vm[pick]
        if r == 0:
            arrived[0] = row
        else:
            stage[r] = row

    row_place = lax.broadcasted_iota(jnp.int32, (rows, 128), 0) // heads
    parity = jnp.zeros((rows, 128), jnp.int32)
    for r in range(n_own):
        source = lax.rem(z - r + n_own, n_own)
        first = (source * n_slice + x) * per_dev
        odd = jnp.int32(0)
        for j in range(per_dev):
            slot = ps_ref[sp_ref[first + j]]
            odd = jnp.where((slot >> 1) == z, slot & 1, odd)
        parity = jnp.where(row_place == r, odd, parity)
    is_odd = parity[:, :1] > 0

    load_suffix.wait()
    suf_tokens = suf_vm.shape[1]
    token = lax.broadcasted_iota(jnp.int32, (heads, suf_tokens), 1)
    for j in range(per_dev):
        recent = suf_vm[j]
        s = lax.dot_general(q_vm[j], recent, NT, preferred_element_type=F32) * scaling
        s = jnp.where(token < sl_ref[j], s, -1e30)
        m = jnp.max(s, axis=1, keepdims=True)
        p = jnp.exp(s - m)
        suf_top[j] = jnp.broadcast_to(m, (heads, 128))
        suf_tot[j] = jnp.broadcast_to(jnp.sum(p, axis=1, keepdims=True), (heads, 128))
        suf_out[j] = jnp.dot(p.astype(BF16), recent[:, :DL], preferred_element_type=F32)

    load_cache.wait()
    pl.semaphore_wait(barrier, n_own - 1 + 3)

    last = n_slice // 2

    def slot_of(side, d):
        if d == 0:
            return 0
        if d == last:
            return n_slice - 1
        return 2 * d - 1 + side

    def part(side, d, piece):
        return keys.at[h, slot_of(side, d), pl.ds(piece * half, half), :]

    def pieces(side, d):
        order = (0, 1) if side == 0 else (1, 0)
        return order[:1] if d == last else order

    started = []

    def ring(side, d, piece):
        at = (side * last + d - 1) * 2 + piece
        return pltpu.make_async_remote_copy(
            src_ref=part(side, d - 1, piece),
            dst_ref=part(side, d, piece),
            send_sem=ring_send.at[at],
            recv_sem=ring_recv.at[at],
            device_id={"sample": right if side == 0 else left},
            device_id_type=MESH,
        )

    def pair(side, d, piece):
        at = (side * last + d - 1) * 2 + piece
        return pltpu.make_async_remote_copy(
            src_ref=part(side, d, piece),
            dst_ref=part(side, d, piece),
            send_sem=pair_send.at[at],
            recv_sem=pair_recv.at[at],
            device_id={"head": partner},
            device_id_type=MESH,
        )

    def pair_in(side, d, piece):
        at = (side * last + d - 1) * 2 + piece
        theirs = keys.at[partner, slot_of(side, d), pl.ds(piece * half, half), :]
        return pltpu.make_async_remote_copy(
            src_ref=theirs,
            dst_ref=theirs,
            send_sem=pair_send.at[at],
            recv_sem=pair_recv.at[at],
            device_id={"head": partner},
            device_id_type=MESH,
        )

    def start(copy):
        copy.start()
        started.append(copy)

    def start_ring(d):
        for k in range(len(pieces(0, d))):
            for side in (0, 1):
                start(ring(side, d, pieces(side, d)[k]))

    def service(d):
        for k in range(len(pieces(0, d))):
            for side in (0, 1):
                piece = pieces(side, d)[k]
                ring(side, d, piece).wait_recv()
                if d < last and piece in pieces(side, d + 1):
                    start(ring(side, d + 1, piece))
                start(pair(side, d, piece))

    def settle(d):
        for k in range(len(pieces(0, d))):
            for side in (0, 1):
                pair_in(side, d, pieces(side, d)[k]).wait_recv()

    def ask(r):
        return pltpu.make_async_remote_copy(
            src_ref=stage.at[r],
            dst_ref=arrived.at[r],
            send_sem=q_send.at[r],
            recv_sem=q_recv.at[r],
            device_id={"prompt": lax.rem(z + r, n_own)},
            device_id_type=MESH,
        )

    def answer(r):
        return pltpu.make_async_remote_copy(
            src_ref=res.at[r],
            dst_ref=ret.at[r],
            send_sem=r_send.at[r],
            recv_sem=r_recv.at[r],
            device_id={"prompt": lax.rem(z - r + n_own, n_own)},
            device_id_type=MESH,
        )

    def answer_stat(r):
        return pltpu.make_async_remote_copy(
            src_ref=stat.at[r],
            dst_ref=ret_stat.at[r],
            send_sem=s_send.at[r],
            recv_sem=s_recv.at[r],
            device_id={"prompt": lax.rem(z - r + n_own, n_own)},
            device_id_type=MESH,
        )

    start_ring(1)
    for r in far_first(n_own):
        start(ask(r))

    def attend(slots, first):
        q = asked[...]
        s0 = [jnp.dot(q, keys[0, k], preferred_element_type=F32) for k in slots]
        s1 = [jnp.dot(q, keys[1, k], preferred_element_type=F32) for k in slots]
        s = [jnp.where(is_odd, b, a) * scaling for a, b in zip(s0, s1)]
        m = functools.reduce(jnp.maximum, [jnp.max(a, axis=1, keepdims=True) for a in s])
        if not first:
            old = top[:, :1]
            m = jnp.maximum(m, old)
            fade = jnp.exp(old - m)
        p = [jnp.exp(a - m) for a in s]
        l = sum(jnp.sum(a, axis=1, keepdims=True) for a in p)
        out = 0.0
        for a, k in zip(p, slots):
            even = jnp.where(is_odd, 0.0, a).astype(BF16)
            odd = jnp.where(is_odd, a, 0.0).astype(BF16)
            out = out + lax.dot_general(even, keys[0, k, :DL], NT, preferred_element_type=F32)
            out = out + lax.dot_general(odd, keys[1, k, :DL], NT, preferred_element_type=F32)
        if not first:
            l = l + tot[:, :1] * fade
            out = out + acc[...] * fade
        top[...] = jnp.broadcast_to(m, (rows, 128))
        tot[...] = jnp.broadcast_to(l, (rows, 128))
        acc[...] = out

    def gather_asked():
        for r in far_first(n_own):
            ask(r).wait_recv()
        asked[...] = arrived[...].reshape(rows, feat)

    for d in range(1, last + 1):
        service(d)
        if d == max(1, last - 2):
            gather_asked()
            attend([0], True)
        if d < last and d >= max(1, last - 2):
            for e in range(1 if d == max(1, last - 2) else d, d + 1):
                settle(e)
                attend([2 * e - 1, 2 * e], False)
    settle(last)
    attend([n_slice - 1], False)

    m = top[...]
    l = tot[...]
    lane = lax.broadcasted_iota(jnp.int32, (rows, 128), 1)
    sub = lax.rem(lax.broadcasted_iota(jnp.int32, (rows, 128), 0), heads)
    both = jnp.where(lane == sub, m, 0.0) + jnp.where(lane == sub + heads, l, 0.0)
    both = jnp.sum(both.reshape(n_own, heads, 128), axis=1)
    for r in range(n_own):
        line = both[r : r + 1, :]
        block = acc[r * heads : (r + 1) * heads, :].astype(BF16)
        if r == 0:
            ret_stat[0] = line
            ret[0] = block
        else:
            stat[r] = line
            res[r] = block
    for r in far_first(n_own):
        start(answer(r))
        start(answer_stat(r))
    for r in far_first(n_own):
        answer(r).wait_recv()
        answer_stat(r).wait_recv()

    lane8 = lax.broadcasted_iota(jnp.int32, (heads, 128), 1)
    sub8 = lax.broadcasted_iota(jnp.int32, (heads, 128), 0)
    for j in range(per_dev):
        line = jnp.broadcast_to(ret_stat[places[j]], (heads, 128))
        pre_top = jnp.sum(jnp.where(lane8 == sub8, line, 0.0), axis=1, keepdims=True)
        pre_tot = jnp.sum(jnp.where(lane8 == sub8 + heads, line, 0.0), axis=1, keepdims=True)
        own_top = suf_top[j][:, :1]
        own_tot = suf_tot[j][:, :1]
        m = jnp.maximum(pre_top, own_top)
        w_pre = jnp.exp(pre_top - m)
        w_own = jnp.exp(own_top - m)
        total = w_pre * pre_tot + w_own * own_tot
        num = w_pre * ret[places[j]].astype(F32) + w_own * suf_out[j]
        out_ref[j] = (num / total).astype(out_ref.dtype)

    for copy in started:
        copy.wait_send()


def solution(mesh):
    n_own = mesh.shape["prompt"]
    n_slice = mesh.shape["sample"]

    def body(queries, prompt_cache, suffix_cache, suffix_len, sample_prompt, prompt_slot):
        per_dev, heads, feat = queries.shape
        tok = prompt_cache.shape[1]
        rows = n_own * heads
        ring = n_slice * 2
        dma = pltpu.SemaphoreType.DMA
        return pl.pallas_call(
            functools.partial(kernel, n_own, n_slice),
            out_shape=jax.ShapeDtypeStruct((per_dev, heads, DL), BF16),
            in_specs=[pl.BlockSpec(memory_space=pltpu.SMEM)] * 3
            + [pl.BlockSpec(memory_space=pl.ANY)] * 3,
            out_specs=pl.BlockSpec(memory_space=pltpu.VMEM),
            scratch_shapes=[
                pltpu.VMEM(queries.shape, BF16),
                pltpu.VMEM((P_DEV, n_slice, feat, tok), BF16),
                pltpu.VMEM(suffix_cache.shape, BF16),
                pltpu.VMEM((n_own, heads, feat), BF16),
                pltpu.VMEM((n_own, heads, feat), BF16),
                pltpu.VMEM((rows, feat), BF16),
                pltpu.VMEM((rows, DL), F32),
                pltpu.VMEM((rows, 128), F32),
                pltpu.VMEM((rows, 128), F32),
                pltpu.VMEM((n_own, heads, DL), BF16),
                pltpu.VMEM((n_own, 1, 128), F32),
                pltpu.VMEM((n_own, heads, DL), BF16),
                pltpu.VMEM((n_own, 1, 128), F32),
                pltpu.VMEM((per_dev, heads, DL), F32),
                pltpu.VMEM((per_dev, heads, 128), F32),
                pltpu.VMEM((per_dev, heads, 128), F32),
                dma((3,)),
                dma((ring,)),
                dma((ring,)),
                dma((ring,)),
                dma((ring,)),
                dma((n_own,)),
                dma((n_own,)),
                dma((n_own,)),
                dma((n_own,)),
                dma((n_own,)),
                dma((n_own,)),
            ],
            compiler_params=pltpu.CompilerParams(collective_id=0, has_side_effects=True),
        )(
            sample_prompt,
            prompt_slot,
            suffix_len,
            queries,
            jnp.swapaxes(prompt_cache, 1, 2),
            suffix_cache,
        )

    return jax.shard_map(
        body,
        mesh=mesh,
        in_specs=(
            P(("groups", "prompt", "sample"), "head", None),
            P(("groups", "prompt"), "sample", None),
            P(("groups", "prompt", "sample"), None, None),
            P(("groups", "prompt", "sample")),
            P("groups"),
            P("groups"),
        ),
        out_specs=P(("groups", "prompt", "sample"), "head", None),
        check_vma=False,
    )
```

time: 302 us -> 80.8 us (0.27); the launches traced: 297 us -> 80.6 us
  waiting for transfers between devices: 161 us -> 0 us
  Pallas kernels: 0 us -> 79.2 us
  starting transfers between devices: 71.5 us -> 0 us
  other arithmetic: 32.8 us -> 0 us
  local copies, waits for them, and re-layouts: 29.5 us -> 1.38 us
    all_to_all x2 -> x0, waiting for transfers between devices: 161 us -> none  [the longest x1 111 us: side_by_side(): lax.all_to_all(both, axis, split_axis=split_dim, concat_axis=concat_dim,...]
    pallas_call x0 -> x1, Pallas kernels: none -> 79.2 us  [body(): pl.pallas_call(functools.partial(kernel, n_own, n_slice), out_shape=jax.S...]
    all_to_all x2 -> x0, starting transfers between devices: 71.5 us -> none  [the longest x1 55.2 us: body(): lax.all_to_all(fanned, ('prompt', 'sample'), split_axis=0, concat_axis=0,...]
    select_n x11 -> x0, other arithmetic: 21.1 us -> none  [the longest x1 20.8 us: routing_tables(): local_prompt = slot_index % P_DEV]
    gather x12 -> x0, local copies, waits for them, and re-layouts: 11.2 us -> none  [the longest x2 3.92 us: routing_tables(): slot_index = jnp.take(prompt_slot, sample_prompt)]
    unnamed x25 -> x1, local copies, waits for them, and re-layouts: 8.99 us -> 1.38 us
    reshape x4 -> x0, local copies, waits for them, and re-layouts: 3.32 us -> none  [the longest x2 2.42 us: side_by_side(): a.reshape(*a.shape[:along], w)]
  transfers between devices with their start and end apart: 2 -> 0, of which waited for: 2 -> 0; matrix products, arithmetic and copies ran while one was open for 2% -> 0% of each run, Pallas kernels for 0% -> 0%
where the time goes in v1:
time: 80.8 us; the launch traced here: 80.6 us
  Pallas kernels  79.2 us (98%)
  local copies, waits for them, and re-layouts  1.38 us (2%)
    pallas_call x1, Pallas kernels, body(): pl.pallas_call(functools.partial(kernel, n_own, n_slice), out_shape=jax.S...  79.2 us

profile of v1, /device:TPU:65, one launch (start us, length us, event | category | flops | bytes accessed | tf_op | source)
XLA Modules:
  0.0 80.6 jit_solution(5103564490981955050)
XLA Ops:
  0.0 79.2 %shard_map.64 = bf16[4,8,512]{2,1,0:T(8,128)(2,1)} custom-call(s32[512]{0:T(512)} %sp_ref.1, s32[32]{0:T(128)} %ps_ref.1, s32[4]{0:T(128)} %sl_ref.1, bf16[4,8,576]{2,1,0:T(8,128)(2,1)} %q_hbm.1, bf16[2,576,128]{2,1,0:T(8,128)(2,1)} %bitcast.1, bf16[4,64,576]{2,1,0:T(8,128)(2,1)} %suffix_hbm.1), custom_call_target="tpu_custom_call" | custom-call | tf_op jit(solution)/shard_map/pallas_call | solution.py:338
  79.2 1.4 %copy.8 = bf16[4,8,512]{2,1,0:T(8,128)(2,1)} copy(bf16[4,8,512]{2,1,0:T(8,128)(2,1)} %shard_map.64) | data formatting | bytes 65536

commit v2 on v1

v2 whole, which is shorter than its diff:
```python
import functools
import math

import jax
import jax.numpy as jnp
from jax import lax
from jax.experimental import pallas as pl
from jax.experimental.pallas import tpu as pltpu
from jax.sharding import PartitionSpec as P

DL = 512
DR = 64
QKN = 128
P_DEV = 2
PIECES = 2
MESH = pl.DeviceIdType.MESH
NT = (((1,), (1,)), ((), ()))
F32 = jnp.float32
BF16 = jnp.bfloat16


def far_first(n):
    return sorted(range(1, n), key=lambda r: -min(r, n - r))


def kernel(
    n_own,
    n_slice,
    sp_hbm,
    ps_hbm,
    sl_hbm,
    q_hbm,
    cache_hbm,
    suffix_hbm,
    out_ref,
    sp_ref,
    ps_ref,
    sl_ref,
    q_vm,
    q_pair,
    keys,
    suf_vm,
    stage,
    arrived,
    asked,
    res,
    stat,
    ret,
    ret_stat,
    suf_out,
    suf_top,
    suf_tot,
    local_sem,
    ring_send,
    ring_recv,
    pair_send,
    pair_recv,
    raw_send,
    raw_recv,
    half_send,
    half_recv,
    q_send,
    q_recv,
    r_send,
    r_recv,
    s_send,
    s_recv,
):
    per_dev, heads, feat = q_vm.shape
    tok = cache_hbm.shape[2]
    rows = n_own * heads
    scaling = 1.0 / math.sqrt(QKN + DR)
    z = lax.axis_index("prompt")
    x = lax.axis_index("sample")
    h = lax.axis_index("head")
    right = lax.rem(x + 1, n_slice)
    left = lax.rem(x + n_slice - 1, n_slice)
    partner = 1 - h
    is_ring = h == 1
    is_post = h == 0

    loads = [
        pltpu.make_async_copy(cache_hbm, keys.at[:, :, pl.ds(0, tok)], local_sem.at[0]),
        pltpu.make_async_copy(q_hbm, q_vm, local_sem.at[1]),
        pltpu.make_async_copy(sp_hbm, sp_ref, local_sem.at[2]),
        pltpu.make_async_copy(ps_hbm, ps_ref, local_sem.at[3]),
        pltpu.make_async_copy(sl_hbm, sl_ref, local_sem.at[4]),
        pltpu.make_async_copy(suffix_hbm, suf_vm, local_sem.at[5]),
    ]
    for load in loads:
        load.start()

    barrier = pltpu.get_barrier_semaphore()
    pl.semaphore_signal(barrier, inc=1, device_id={"head": partner}, device_id_type=MESH)

    @pl.when(is_ring)
    def _():
        pl.semaphore_signal(barrier, inc=1, device_id={"sample": right}, device_id_type=MESH)
        pl.semaphore_signal(barrier, inc=1, device_id={"sample": left}, device_id_type=MESH)

    @pl.when(is_post)
    def _():
        for r in far_first(n_own):
            pl.semaphore_signal(
                barrier, inc=1, device_id={"prompt": lax.rem(z + r, n_own)}, device_id_type=MESH
            )

    last = n_slice // 2
    half = feat // PIECES

    def slot_of(side, d):
        if d == 0:
            return 0
        if d == last:
            return n_slice - 1
        return 2 * d - 1 + side

    def pieces(side, d):
        order = [side, 1 - side][: 1 if d == last else 2]
        return [(p, f) for p in order for f in range(PIECES)]

    def part(side, d, piece):
        p, f = piece
        return keys.at[p, pl.ds(f * half, half), pl.ds(slot_of(side, d) * tok, tok)]

    def sem_at(side, d, piece):
        p, f = piece
        return ((side * last + d - 1) * P_DEV + p) * PIECES + f

    def ring(side, d, piece):
        at = sem_at(side, d, piece)
        return pltpu.make_async_remote_copy(
            src_ref=part(side, d - 1, piece),
            dst_ref=part(side, d, piece),
            send_sem=ring_send.at[at],
            recv_sem=ring_recv.at[at],
            device_id={"sample": right if side == 0 else left},
            device_id_type=MESH,
        )

    def pair(side, d, piece):
        at = sem_at(side, d, piece)
        return pltpu.make_async_remote_copy(
            src_ref=part(side, d, piece),
            dst_ref=part(side, d, piece),
            send_sem=pair_send.at[at],
            recv_sem=pair_recv.at[at],
            device_id={"head": partner},
            device_id_type=MESH,
        )

    def every_piece():
        for d in range(1, last + 1):
            for k in range(len(pieces(0, d))):
                for side in (0, 1):
                    yield side, d, pieces(side, d)[k]

    def raw():
        return pltpu.make_async_remote_copy(
            src_ref=q_vm,
            dst_ref=q_pair,
            send_sem=raw_send.at[0],
            recv_sem=raw_recv.at[0],
            device_id={"head": partner},
            device_id_type=MESH,
        )

    def hand(r):
        return pltpu.make_async_remote_copy(
            src_ref=arrived.at[r, 1],
            dst_ref=arrived.at[r, 1],
            send_sem=half_send.at[r],
            recv_sem=half_recv.at[r],
            device_id={"head": partner},
            device_id_type=MESH,
        )

    def ask(r):
        return pltpu.make_async_remote_copy(
            src_ref=stage.at[r],
            dst_ref=arrived.at[r],
            send_sem=q_send.at[r],
            recv_sem=q_recv.at[r],
            device_id={"prompt": lax.rem(z + r, n_own)},
            device_id_type=MESH,
        )

    def answer(r):
        return pltpu.make_async_remote_copy(
            src_ref=res.at[r],
            dst_ref=ret.at[r],
            send_sem=r_send.at[r],
            recv_sem=r_recv.at[r],
            device_id={"prompt": lax.rem(z - r + n_own, n_own)},
            device_id_type=MESH,
        )

    def answer_stat(r):
        return pltpu.make_async_remote_copy(
            src_ref=stat.at[r],
            dst_ref=ret_stat.at[r],
            send_sem=s_send.at[r],
            recv_sem=s_recv.at[r],
            device_id={"prompt": lax.rem(z - r + n_own, n_own)},
            device_id_type=MESH,
        )

    own = (z * n_slice + x) * per_dev

    def own_places():
        return [
            lax.rem((ps_ref[sp_ref[own + j]] >> 1) - z + n_own, n_own) for j in range(per_dev)
        ]

    @pl.when(is_ring)
    def _():
        loads[1].wait()
        loads[0].wait()
        pl.semaphore_wait(barrier, 3)
        raw().start()
        for k in range(len(pieces(0, 1))):
            for side in (0, 1):
                ring(side, 1, pieces(side, 1)[k]).start()
        loads[2].wait()
        loads[3].wait()

    @pl.when(is_post)
    def _():
        loads[1].wait()
        loads[2].wait()
        loads[3].wait()
        picks = own_places()

        def row_of(r):
            pick = jnp.int32(0)
            for j in range(1, per_dev):
                pick = jnp.where(picks[j] == r, j, pick)
            return pick

        for r in far_first(n_own) + [0]:
            stage[r, 0] = q_vm[row_of(r)]
        pl.semaphore_wait(barrier, n_own)
        raw().wait_recv()
        for r in far_first(n_own) + [0]:
            stage[r, 1] = q_pair[row_of(r)]
        for r in far_first(n_own):
            ask(r).start()
        arrived[0] = stage[0]
        hand(0).start()
        loads[0].wait()

    loads[4].wait()
    loads[5].wait()
    suf_tokens = suf_vm.shape[1]
    token = lax.broadcasted_iota(jnp.int32, (heads, suf_tokens), 1)
    for j in range(per_dev):
        recent = suf_vm[j]
        s = lax.dot_general(q_vm[j], recent, NT, preferred_element_type=F32) * scaling
        s = jnp.where(token < sl_ref[j], s, -1e30)
        m = jnp.max(s, axis=1, keepdims=True)
        p = jnp.exp(s - m)
        suf_top[j] = jnp.broadcast_to(m, (heads, 128))
        suf_tot[j] = jnp.broadcast_to(jnp.sum(p, axis=1, keepdims=True), (heads, 128))
        suf_out[j] = jnp.dot(p.astype(BF16), recent[:, :DL], preferred_element_type=F32)

    row_place = lax.broadcasted_iota(jnp.int32, (rows, 128), 0) // heads
    parity = jnp.zeros((rows, 128), jnp.int32)
    for r in range(n_own):
        source = lax.rem(z - r + n_own, n_own)
        first = (source * n_slice + x) * per_dev
        odd = jnp.int32(0)
        for j in range(per_dev):
            slot = ps_ref[sp_ref[first + j]]
            odd = jnp.where((slot >> 1) == z, slot & 1, odd)
        parity = jnp.where(row_place == r, odd, parity)

    @pl.when(is_ring)
    def _():
        for side, d, piece in every_piece():
            ring(side, d, piece).wait_recv()
            if d < last and piece in pieces(side, d + 1):
                ring(side, d + 1, piece).start()
            pair(side, d, piece).start()
        for r in far_first(n_own)[::-1] + [0]:
            hand(r).wait_recv()
        asked[...] = arrived[:, 1].reshape(rows, feat)

    @pl.when(is_post)
    def _():
        for r in far_first(n_own)[::-1]:
            ask(r).wait_recv()
            hand(r).start()
        asked[...] = arrived[:, 0].reshape(rows, feat)
        for side, d, piece in every_piece():
            pair(side, d, piece).wait_recv()

    is_odd = parity[:, :1] > 0
    q = asked[...]
    s0 = jnp.dot(q, keys[0], preferred_element_type=F32)
    s1 = jnp.dot(q, keys[1], preferred_element_type=F32)
    s = jnp.where(is_odd, s1, s0) * scaling
    m = jnp.max(s, axis=1, keepdims=True)
    p = jnp.exp(s - m)
    l = jnp.sum(p, axis=1, keepdims=True)
    out = lax.dot_general(
        jnp.where(is_odd, 0.0, p).astype(BF16), keys[0, :DL], NT, preferred_element_type=F32
    ) + lax.dot_general(
        jnp.where(is_odd, p, 0.0).astype(BF16), keys[1, :DL], NT, preferred_element_type=F32
    )

    lane = lax.broadcasted_iota(jnp.int32, (rows, 128), 1)
    sub = lax.rem(lax.broadcasted_iota(jnp.int32, (rows, 128), 0), heads)
    both = jnp.where(lane == sub, m, 0.0) + jnp.where(lane == sub + heads, l, 0.0)
    both = jnp.sum(both.reshape(n_own, heads, 128), axis=1)
    for r in range(n_own):
        line = both[r : r + 1, :]
        block = out[r * heads : (r + 1) * heads, :].astype(BF16)
        if r == 0:
            ret_stat[0] = line
            ret[0] = block
        else:
            stat[r] = line
            res[r] = block
    for r in far_first(n_own):
        answer(r).start()
        answer_stat(r).start()

    places = own_places()
    for r in far_first(n_own)[::-1]:
        answer(r).wait_recv()
        answer_stat(r).wait_recv()

    lane8 = lax.broadcasted_iota(jnp.int32, (heads, 128), 1)
    sub8 = lax.broadcasted_iota(jnp.int32, (heads, 128), 0)
    for j in range(per_dev):
        line = jnp.broadcast_to(ret_stat[places[j]], (heads, 128))
        pre_top = jnp.sum(jnp.where(lane8 == sub8, line, 0.0), axis=1, keepdims=True)
        pre_tot = jnp.sum(jnp.where(lane8 == sub8 + heads, line, 0.0), axis=1, keepdims=True)
        own_top = suf_top[j][:, :1]
        own_tot = suf_tot[j][:, :1]
        m = jnp.maximum(pre_top, own_top)
        w_pre = jnp.exp(pre_top - m)
        w_own = jnp.exp(own_top - m)
        total = w_pre * pre_tot + w_own * own_tot
        num = w_pre * ret[places[j]].astype(F32) + w_own * suf_out[j]
        out_ref[j] = (num / total).astype(out_ref.dtype)

    for r in far_first(n_own):
        answer(r).wait_send()
        answer_stat(r).wait_send()

    @pl.when(is_ring)
    def _():
        raw().wait_send()
        for side, d, piece in every_piece():
            ring(side, d, piece).wait_send()
            pair(side, d, piece).wait_send()

    @pl.when(is_post)
    def _():
        for r in far_first(n_own):
            ask(r).wait_send()
        for r in range(n_own):
            hand(r).wait_send()


def solution(mesh):
    n_own = mesh.shape["prompt"]
    n_slice = mesh.shape["sample"]

    def body(queries, prompt_cache, suffix_cache, suffix_len, sample_prompt, prompt_slot):
        per_dev, heads, feat = queries.shape
        tok = prompt_cache.shape[1]
        rows = n_own * heads
        ring = n_slice * P_DEV * PIECES
        dma = pltpu.SemaphoreType.DMA
        return pl.pallas_call(
            functools.partial(kernel, n_own, n_slice),
            out_shape=jax.ShapeDtypeStruct((per_dev, heads, DL), BF16),
            in_specs=[pl.BlockSpec(memory_space=pl.ANY)] * 6,
            out_specs=pl.BlockSpec(memory_space=pltpu.VMEM),
            scratch_shapes=[
                pltpu.SMEM(sample_prompt.shape, jnp.int32),
                pltpu.SMEM(prompt_slot.shape, jnp.int32),
                pltpu.SMEM(suffix_len.shape, jnp.int32),
                pltpu.VMEM(queries.shape, BF16),
                pltpu.VMEM(queries.shape, BF16),
                pltpu.VMEM((P_DEV, feat, n_slice * tok), BF16),
                pltpu.VMEM(suffix_cache.shape, BF16),
                pltpu.VMEM((n_own, 2, heads, feat), BF16),
                pltpu.VMEM((n_own, 2, heads, feat), BF16),
                pltpu.VMEM((rows, feat), BF16),
                pltpu.VMEM((n_own, heads, DL), BF16),
                pltpu.VMEM((n_own, 1, 128), F32),
                pltpu.VMEM((n_own, heads, DL), BF16),
                pltpu.VMEM((n_own, 1, 128), F32),
                pltpu.VMEM((per_dev, heads, DL), F32),
                pltpu.VMEM((per_dev, heads, 128), F32),
                pltpu.VMEM((per_dev, heads, 128), F32),
                dma((6,)),
                dma((ring,)),
                dma((ring,)),
                dma((ring,)),
                dma((ring,)),
                dma((1,)),
                dma((1,)),
                dma((n_own,)),
                dma((n_own,)),
                dma((n_own,)),
                dma((n_own,)),
                dma((n_own,)),
                dma((n_own,)),
                dma((n_own,)),
                dma((n_own,)),
            ],
            compiler_params=pltpu.CompilerParams(collective_id=0, has_side_effects=True),
        )(
            sample_prompt,
            prompt_slot,
            suffix_len,
            queries,
            jnp.swapaxes(prompt_cache, 1, 2),
            suffix_cache,
        )

    return jax.shard_map(
        body,
        mesh=mesh,
        in_specs=(
            P(("groups", "prompt", "sample"), "head", None),
            P(("groups", "prompt"), "sample", None),
            P(("groups", "prompt", "sample"), None, None),
            P(("groups", "prompt", "sample")),
            P("groups"),
            P("groups"),
        ),
        out_specs=P(("groups", "prompt", "sample"), "head", None),
        check_vma=False,
    )
```

time: 80.8 us -> 74.7 us (0.925)
  Pallas kernels: 79.2 us -> 73.1 us
    pallas_call x1, Pallas kernels: 79.2 us -> 73.1 us  [body(): pl.pallas_call(functools.partial(kernel, n_own, n_slice), out_shape=jax.S...]
where the time goes in v2:
time: 74.7 us; the launch traced here: 74.5 us
  Pallas kernels  73.1 us (98%)
  local copies, waits for them, and re-layouts  1.38 us (2%)
    pallas_call x1, Pallas kernels, body(): pl.pallas_call(functools.partial(kernel, n_own, n_slice), out_shape=jax.S...  73.1 us

profile of v2, /device:TPU:65, one launch (start us, length us, event | category | flops | bytes accessed | tf_op | source)
XLA Modules:
  0.0 74.5 jit_solution(9019585891249319235)
XLA Ops:
  0.0 73.1 %shard_map.64 = bf16[4,8,512]{2,1,0:T(8,128)(2,1)} custom-call(s32[512]{0:T(512)} %sp_hbm.1, s32[32]{0:T(128)} %ps_hbm.1, s32[4]{0:T(128)} %sl_hbm.1, bf16[4,8,576]{2,1,0:T(8,128)(2,1)} %q_hbm.1, bf16[2,576,128]{2,1,0:T(8,128)(2,1)} %bitcast.1, bf16[4,64,576]{2,1,0:T(8,128)(2,1)} %suffix_hbm.1), custom_call_target="tpu_custom_call" | custom-call | tf_op jit(solution)/shard_map/pallas_call | solution.py:377
  73.1 1.4 %copy.8 = bf16[4,8,512]{2,1,0:T(8,128)(2,1)} copy(bf16[4,8,512]{2,1,0:T(8,128)(2,1)} %shard_map.64) | data formatting | bytes 65536

commit v3 on v2

--- a/solution.py
+++ b/solution.py
@@ -12,6 +12,7 @@
 DR = 64
 QKN = 128
 P_DEV = 2
+POST = 0
 PIECES = 2
 MESH = pl.DeviceIdType.MESH
 NT = (((1,), (1,)), ((), ()))
@@ -42,7 +43,6 @@
     suf_vm,
     stage,
     arrived,
-    asked,
     res,
     stat,
     ret,
@@ -57,8 +57,6 @@
     pair_recv,
     raw_send,
     raw_recv,
-    half_send,
-    half_recv,
     q_send,
     q_recv,
     r_send,
@@ -76,8 +74,8 @@
     right = lax.rem(x + 1, n_slice)
     left = lax.rem(x + n_slice - 1, n_slice)
     partner = 1 - h
-    is_ring = h == 1
-    is_post = h == 0
+    is_ring = h != POST
+    is_post = h == POST
 
     loads = [
         pltpu.make_async_copy(cache_hbm, keys.at[:, :, pl.ds(0, tok)], local_sem.at[0]),
@@ -97,6 +95,13 @@
     def _():
         pl.semaphore_signal(barrier, inc=1, device_id={"sample": right}, device_id_type=MESH)
         pl.semaphore_signal(barrier, inc=1, device_id={"sample": left}, device_id_type=MESH)
+        for r in far_first(n_own):
+            pl.semaphore_signal(
+                barrier,
+                inc=1,
+                device_id={"prompt": lax.rem(z + r, n_own), "head": POST},
+                device_id_type=MESH,
+            )
 
     @pl.when(is_post)
     def _():
@@ -165,23 +170,26 @@
             device_id_type=MESH,
         )
 
-    def hand(r):
-        return pltpu.make_async_remote_copy(
-            src_ref=arrived.at[r, 1],
-            dst_ref=arrived.at[r, 1],
-            send_sem=half_send.at[r],
-            recv_sem=half_recv.at[r],
+    def hand():
+        return pltpu.make_async_remote_copy(
+            src_ref=stage.at[1, 0],
+            dst_ref=arrived.at[0],
+            send_sem=q_send.at[1, 0],
+            recv_sem=q_recv.at[0],
             device_id={"head": partner},
             device_id_type=MESH,
         )
 
-    def ask(r):
-        return pltpu.make_async_remote_copy(
-            src_ref=stage.at[r],
+    def ask(side, r):
+        return pltpu.make_async_remote_copy(
+            src_ref=stage.at[side, r],
             dst_ref=arrived.at[r],
-            send_sem=q_send.at[r],
+            send_sem=q_send.at[side, r],
             recv_sem=q_recv.at[r],
-            device_id={"prompt": lax.rem(z + r, n_own)},
+            device_id={
+                "prompt": lax.rem(z + r, n_own),
+                "head": POST if side == 0 else 1 - POST,
+            },
             device_id_type=MESH,
         )
 
@@ -238,15 +246,17 @@
             return pick
 
         for r in far_first(n_own) + [0]:
-            stage[r, 0] = q_vm[row_of(r)]
-        pl.semaphore_wait(barrier, n_own)
+            stage[0, r] = q_vm[row_of(r)]
+        arrived[0] = stage[0, 0]
+        pl.semaphore_wait(barrier, 2 * n_own - 1)
+        for r in far_first(n_own):
+            ask(0, r).start()
         raw().wait_recv()
         for r in far_first(n_own) + [0]:
-            stage[r, 1] = q_pair[row_of(r)]
+            stage[1, r] = q_pair[row_of(r)]
         for r in far_first(n_own):
-            ask(r).start()
-        arrived[0] = stage[0]
-        hand(0).start()
+            ask(1, r).start()
+        hand().start()
         loads[0].wait()
 
     loads[4].wait()
@@ -281,21 +291,18 @@
             if d < last and piece in pieces(side, d + 1):
                 ring(side, d + 1, piece).start()
             pair(side, d, piece).start()
-        for r in far_first(n_own)[::-1] + [0]:
-            hand(r).wait_recv()
-        asked[...] = arrived[:, 1].reshape(rows, feat)
+        hand().wait_recv()
 
     @pl.when(is_post)
     def _():
-        for r in far_first(n_own)[::-1]:
-            ask(r).wait_recv()
-            hand(r).start()
-        asked[...] = arrived[:, 0].reshape(rows, feat)
         for side, d, piece in every_piece():
             pair(side, d, piece).wait_recv()
 
+    for r in far_first(n_own)[::-1]:
+        ask(0, r).wait_recv()
+
     is_odd = parity[:, :1] > 0
-    q = asked[...]
+    q = arrived[...].reshape(rows, feat)
     s0 = jnp.dot(q, keys[0], preferred_element_type=F32)
     s1 = jnp.dot(q, keys[1], preferred_element_type=F32)
     s = jnp.where(is_odd, s1, s0) * scaling
@@ -359,9 +366,9 @@
     @pl.when(is_post)
     def _():
         for r in far_first(n_own):
-            ask(r).wait_send()
-        for r in range(n_own):
-            hand(r).wait_send()
+            ask(0, r).wait_send()
+            ask(1, r).wait_send()
+        hand().wait_send()
 
 
 def solution(mesh):
@@ -371,13 +378,12 @@
     def body(queries, prompt_cache, suffix_cache, suffix_len, sample_prompt, prompt_slot):
         per_dev, heads, feat = queries.shape
         tok = prompt_cache.shape[1]
-        rows = n_own * heads
         ring = n_slice * P_DEV * PIECES
         dma = pltpu.SemaphoreType.DMA
         return pl.pallas_call(
             functools.partial(kernel, n_own, n_slice),
             out_shape=jax.ShapeDtypeStruct((per_dev, heads, DL), BF16),
-            in_specs=[pl.BlockSpec(memory_space=pl.ANY)] * 6,
+            in_specs=[pl.BlockSpec(memory_space=pltpu.HBM)] * 6,
             out_specs=pl.BlockSpec(memory_space=pltpu.VMEM),
             scratch_shapes=[
                 pltpu.SMEM(sample_prompt.shape, jnp.int32),
@@ -387,9 +393,8 @@
                 pltpu.VMEM(queries.shape, BF16),
                 pltpu.VMEM((P_DEV, feat, n_slice * tok), BF16),
                 pltpu.VMEM(suffix_cache.shape, BF16),
-                pltpu.VMEM((n_own, 2, heads, feat), BF16),
-                pltpu.VMEM((n_own, 2, heads, feat), BF16),
-                pltpu.VMEM((rows, feat), BF16),
+                pltpu.VMEM((2, n_own, heads, feat), BF16),
+                pltpu.VMEM((n_own, heads, feat), BF16),
                 pltpu.VMEM((n_own, heads, DL), BF16),
                 pltpu.VMEM((n_own, 1, 128), F32),
                 pltpu.VMEM((n_own, heads, DL), BF16),
@@ -404,9 +409,7 @@
                 dma((ring,)),
                 dma((1,)),
                 dma((1,)),
-                dma((n_own,)),
-                dma((n_own,)),
-                dma((n_own,)),
+                dma((2, n_own)),
                 dma((n_own,)),
                 dma((n_own,)),
                 dma((n_own,)),

time: 74.7 us -> 71.6 us (0.959)
  Pallas kernels: 73.1 us -> 70 us
    pallas_call x1, Pallas kernels: 73.1 us -> 70 us  [body(): pl.pallas_call(functools.partial(kernel, n_own, n_slice), out_shape=jax.S...]
where the time goes in v3:
time: 71.6 us; the launch traced here: 71.4 us
  Pallas kernels  70 us (98%)
  local copies, waits for them, and re-layouts  1.38 us (2%)
    pallas_call x1, Pallas kernels, body(): pl.pallas_call(functools.partial(kernel, n_own, n_slice), out_shape=jax.S...  70 us

profile of v3, /device:TPU:65, one launch (start us, length us, event | category | flops | bytes accessed | tf_op | source)
XLA Modules:
  0.0 71.4 jit_solution(17091085091720195569)
XLA Ops:
  0.0 70.0 %shard_map.64 = bf16[4,8,512]{2,1,0:T(8,128)(2,1)} custom-call(s32[512]{0:T(512)} %sp_hbm.1, s32[32]{0:T(128)} %ps_hbm.1, s32[4]{0:T(128)} %sl_hbm.1, bf16[4,8,576]{2,1,0:T(8,128)(2,1)} %q_hbm.1, bf16[2,576,128]{2,1,0:T(8,128)(2,1)} %bitcast.1, bf16[4,64,576]{2,1,0:T(8,128)(2,1)} %suffix_hbm.1), custom_call_target="tpu_custom_call" | custom-call | tf_op jit(solution)/shard_map/pallas_call | solution.py:383
  70.0 1.4 %copy.8 = bf16[4,8,512]{2,1,0:T(8,128)(2,1)} copy(bf16[4,8,512]{2,1,0:T(8,128)(2,1)} %shard_map.64) | data formatting | bytes 65536

commit v4 on v3

--- a/solution.py
+++ b/solution.py
@@ -14,6 +14,7 @@
 P_DEV = 2
 POST = 0
 PIECES = 2
+SHARE = 8
 MESH = pl.DeviceIdType.MESH
 NT = (((1,), (1,)), ((), ()))
 F32 = jnp.float32
@@ -50,6 +51,7 @@
     suf_out,
     suf_top,
     suf_tot,
+    parity,
     local_sem,
     ring_send,
     ring_recv,
@@ -172,53 +174,103 @@
 
     def hand():
         return pltpu.make_async_remote_copy(
-            src_ref=stage.at[1, 0],
-            dst_ref=arrived.at[0],
-            send_sem=q_send.at[1, 0],
-            recv_sem=q_recv.at[0],
+            src_ref=stage.at[1, z],
+            dst_ref=arrived.at[z],
+            send_sem=q_send.at[1, z],
+            recv_sem=q_recv.at[z],
             device_id={"head": partner},
             device_id_type=MESH,
         )
 
-    def ask(side, r):
-        return pltpu.make_async_remote_copy(
-            src_ref=stage.at[side, r],
-            dst_ref=arrived.at[r],
-            send_sem=q_send.at[side, r],
-            recv_sem=q_recv.at[r],
-            device_id={
-                "prompt": lax.rem(z + r, n_own),
-                "head": POST if side == 0 else 1 - POST,
-            },
-            device_id_type=MESH,
-        )
-
-    def answer(r):
-        return pltpu.make_async_remote_copy(
-            src_ref=res.at[r],
-            dst_ref=ret.at[r],
-            send_sem=r_send.at[r],
-            recv_sem=r_recv.at[r],
-            device_id={"prompt": lax.rem(z - r + n_own, n_own)},
-            device_id_type=MESH,
-        )
-
-    def answer_stat(r):
-        return pltpu.make_async_remote_copy(
-            src_ref=stat.at[r],
-            dst_ref=ret_stat.at[r],
-            send_sem=s_send.at[r],
-            recv_sem=s_recv.at[r],
-            device_id={"prompt": lax.rem(z - r + n_own, n_own)},
-            device_id_type=MESH,
-        )
+    def ask(side, row):
+        return pltpu.make_async_remote_copy(
+            src_ref=stage.at[side, row],
+            dst_ref=arrived.at[z],
+            send_sem=q_send.at[side, row],
+            recv_sem=q_recv.at[z],
+            device_id={"prompt": row, "head": POST if side == 0 else 1 - POST},
+            device_id_type=MESH,
+        )
+
+    def asked_by(row):
+        return pltpu.make_async_remote_copy(
+            src_ref=stage.at[0, row],
+            dst_ref=arrived.at[row],
+            send_sem=q_send.at[0, row],
+            recv_sem=q_recv.at[row],
+            device_id={"prompt": row},
+            device_id_type=MESH,
+        )
+
+    def answer(row):
+        return pltpu.make_async_remote_copy(
+            src_ref=res.at[row],
+            dst_ref=ret.at[z],
+            send_sem=r_send.at[row],
+            recv_sem=r_recv.at[z],
+            device_id={"prompt": row},
+            device_id_type=MESH,
+        )
+
+    def answer_stat(row):
+        return pltpu.make_async_remote_copy(
+            src_ref=stat.at[row],
+            dst_ref=ret_stat.at[z],
+            send_sem=s_send.at[row],
+            recv_sem=s_recv.at[z],
+            device_id={"prompt": row},
+            device_id_type=MESH,
+        )
+
+    def answered_by(row):
+        return [
+            pltpu.make_async_remote_copy(
+                src_ref=source.at[row],
+                dst_ref=target.at[row],
+                send_sem=send.at[row],
+                recv_sem=recv.at[row],
+                device_id={"prompt": row},
+                device_id_type=MESH,
+            )
+            for source, target, send, recv in (
+                (res, ret, r_send, r_recv),
+                (stat, ret_stat, s_send, s_recv),
+            )
+        ]
 
     own = (z * n_slice + x) * per_dev
 
     def own_places():
-        return [
-            lax.rem((ps_ref[sp_ref[own + j]] >> 1) - z + n_own, n_own) for j in range(per_dev)
-        ]
+        return [ps_ref[sp_ref[own + j]] >> 1 for j in range(per_dev)]
+
+    def others():
+        return [lax.rem(z + r, n_own) for r in far_first(n_own)]
+
+    def recent_part():
+        loads[4].wait()
+        loads[5].wait()
+        suf_tokens = suf_vm.shape[1]
+        token = lax.broadcasted_iota(jnp.int32, (heads, suf_tokens), 1)
+        for j in range(per_dev):
+            recent = suf_vm[j]
+            s = lax.dot_general(q_vm[j], recent, NT, preferred_element_type=F32) * scaling
+            s = jnp.where(token < sl_ref[j], s, -1e30)
+            m = jnp.max(s, axis=1, keepdims=True)
+            p = jnp.exp(s - m)
+            suf_top[j] = jnp.broadcast_to(m, (heads, 128))
+            suf_tot[j] = jnp.broadcast_to(jnp.sum(p, axis=1, keepdims=True), (heads, 128))
+            suf_out[j] = jnp.dot(p.astype(BF16), recent[:, :DL], preferred_element_type=F32)
+
+        row_place = lax.broadcasted_iota(jnp.int32, (rows, 128), 0) // heads
+        odds = jnp.zeros((rows, 128), jnp.int32)
+        for row in range(n_own):
+            first = (row * n_slice + x) * per_dev
+            odd = jnp.int32(0)
+            for j in range(per_dev):
+                slot = ps_ref[sp_ref[first + j]]
+                odd = jnp.where((slot >> 1) == z, slot & 1, odd)
+            odds = jnp.where(row_place == row, odd, odds)
+        parity[...] = odds
 
     @pl.when(is_ring)
     def _():
@@ -231,111 +283,89 @@
                 ring(side, 1, pieces(side, 1)[k]).start()
         loads[2].wait()
         loads[3].wait()
-
-    @pl.when(is_post)
-    def _():
-        loads[1].wait()
-        loads[2].wait()
-        loads[3].wait()
-        picks = own_places()
-
-        def row_of(r):
-            pick = jnp.int32(0)
-            for j in range(1, per_dev):
-                pick = jnp.where(picks[j] == r, j, pick)
-            return pick
-
-        for r in far_first(n_own) + [0]:
-            stage[0, r] = q_vm[row_of(r)]
-        arrived[0] = stage[0, 0]
-        pl.semaphore_wait(barrier, 2 * n_own - 1)
-        for r in far_first(n_own):
-            ask(0, r).start()
-        raw().wait_recv()
-        for r in far_first(n_own) + [0]:
-            stage[1, r] = q_pair[row_of(r)]
-        for r in far_first(n_own):
-            ask(1, r).start()
-        hand().start()
-        loads[0].wait()
-
-    loads[4].wait()
-    loads[5].wait()
-    suf_tokens = suf_vm.shape[1]
-    token = lax.broadcasted_iota(jnp.int32, (heads, suf_tokens), 1)
-    for j in range(per_dev):
-        recent = suf_vm[j]
-        s = lax.dot_general(q_vm[j], recent, NT, preferred_element_type=F32) * scaling
-        s = jnp.where(token < sl_ref[j], s, -1e30)
-        m = jnp.max(s, axis=1, keepdims=True)
-        p = jnp.exp(s - m)
-        suf_top[j] = jnp.broadcast_to(m, (heads, 128))
-        suf_tot[j] = jnp.broadcast_to(jnp.sum(p, axis=1, keepdims=True), (heads, 128))
-        suf_out[j] = jnp.dot(p.astype(BF16), recent[:, :DL], preferred_element_type=F32)
-
-    row_place = lax.broadcasted_iota(jnp.int32, (rows, 128), 0) // heads
-    parity = jnp.zeros((rows, 128), jnp.int32)
-    for r in range(n_own):
-        source = lax.rem(z - r + n_own, n_own)
-        first = (source * n_slice + x) * per_dev
-        odd = jnp.int32(0)
-        for j in range(per_dev):
-            slot = ps_ref[sp_ref[first + j]]
-            odd = jnp.where((slot >> 1) == z, slot & 1, odd)
-        parity = jnp.where(row_place == r, odd, parity)
-
-    @pl.when(is_ring)
-    def _():
+        recent_part()
         for side, d, piece in every_piece():
             ring(side, d, piece).wait_recv()
             if d < last and piece in pieces(side, d + 1):
                 ring(side, d + 1, piece).start()
             pair(side, d, piece).start()
-        hand().wait_recv()
 
     @pl.when(is_post)
     def _():
+        for load in loads[:4]:
+            load.wait()
+        picks = own_places()
+
+        def sample_of(row):
+            pick = jnp.int32(0)
+            for j in range(1, per_dev):
+                pick = jnp.where(picks[j] == row, j, pick)
+            return pick
+
+        for row in range(n_own):
+            stage[0, row] = q_vm[sample_of(row)]
+        recent_part()
+        raw().wait_recv()
+        for row in range(n_own):
+            stage[1, row] = q_pair[sample_of(row)]
+        arrived[z] = stage[0, z]
+        pl.semaphore_wait(barrier, 2 * n_own - 1)
+        for row in others():
+            ask(0, row).start()
+            ask(1, row).start()
+        hand().start()
         for side, d, piece in every_piece():
             pair(side, d, piece).wait_recv()
 
-    for r in far_first(n_own)[::-1]:
-        ask(0, r).wait_recv()
-
-    is_odd = parity[:, :1] > 0
-    q = arrived[...].reshape(rows, feat)
-    s0 = jnp.dot(q, keys[0], preferred_element_type=F32)
-    s1 = jnp.dot(q, keys[1], preferred_element_type=F32)
-    s = jnp.where(is_odd, s1, s0) * scaling
-    m = jnp.max(s, axis=1, keepdims=True)
-    p = jnp.exp(s - m)
-    l = jnp.sum(p, axis=1, keepdims=True)
-    out = lax.dot_general(
-        jnp.where(is_odd, 0.0, p).astype(BF16), keys[0, :DL], NT, preferred_element_type=F32
-    ) + lax.dot_general(
-        jnp.where(is_odd, p, 0.0).astype(BF16), keys[1, :DL], NT, preferred_element_type=F32
-    )
-
-    lane = lax.broadcasted_iota(jnp.int32, (rows, 128), 1)
-    sub = lax.rem(lax.broadcasted_iota(jnp.int32, (rows, 128), 0), heads)
-    both = jnp.where(lane == sub, m, 0.0) + jnp.where(lane == sub + heads, l, 0.0)
-    both = jnp.sum(both.reshape(n_own, heads, 128), axis=1)
-    for r in range(n_own):
-        line = both[r : r + 1, :]
-        block = out[r * heads : (r + 1) * heads, :].astype(BF16)
-        if r == 0:
-            ret_stat[0] = line
-            ret[0] = block
-        else:
-            stat[r] = line
-            res[r] = block
-    for r in far_first(n_own):
-        answer(r).start()
-        answer_stat(r).start()
+    def attend(lo, hi):
+        for row in range(lo, hi):
+
+            @pl.when(jnp.logical_or(is_ring, z != row))
+            def _():
+                asked_by(row).wait_recv()
+
+        size = (hi - lo) * heads
+        is_odd = parity[lo * heads : hi * heads, :1] > 0
+        q = arrived[lo:hi].reshape(size, feat)
+        s0 = jnp.dot(q, keys[0], preferred_element_type=F32)
+        s1 = jnp.dot(q, keys[1], preferred_element_type=F32)
+        s = jnp.where(is_odd, s1, s0) * scaling
+        m = jnp.max(s, axis=1, keepdims=True)
+        p = jnp.exp(s - m)
+        l = jnp.sum(p, axis=1, keepdims=True)
+        out = lax.dot_general(
+            jnp.where(is_odd, 0.0, p).astype(BF16), keys[0, :DL], NT, preferred_element_type=F32
+        ) + lax.dot_general(
+            jnp.where(is_odd, p, 0.0).astype(BF16), keys[1, :DL], NT, preferred_element_type=F32
+        )
+        lane = lax.broadcasted_iota(jnp.int32, (size, 128), 1)
+        sub = lax.rem(lax.broadcasted_iota(jnp.int32, (size, 128), 0), heads)
+        both = jnp.where(lane == sub, m, 0.0) + jnp.where(lane == sub + heads, l, 0.0)
+        both = jnp.sum(both.reshape(hi - lo, heads, 128), axis=1)
+        for row in range(lo, hi):
+            at = row - lo
+            stat[row] = both[at : at + 1, :]
+            res[row] = out[at * heads : (at + 1) * heads, :].astype(BF16)
+        for row in range(lo, hi):
+
+            @pl.when(z != row)
+            def _():
+                answer(row).start()
+                answer_stat(row).start()
+
+    cuts = [0, n_own // SHARE, n_own]
+    for lo, hi in zip(cuts, cuts[1:]):
+        attend(lo, hi)
+    ret[z] = res[z]
+    ret_stat[z] = stat[z]
 
     places = own_places()
-    for r in far_first(n_own)[::-1]:
-        answer(r).wait_recv()
-        answer_stat(r).wait_recv()
+    for row in range(n_own):
+
+        @pl.when(z != row)
+        def _():
+            for copy in answered_by(row):
+                copy.wait_recv()
 
     lane8 = lax.broadcasted_iota(jnp.int32, (heads, 128), 1)
     sub8 = lax.broadcasted_iota(jnp.int32, (heads, 128), 0)
@@ -352,9 +382,9 @@
         num = w_pre * ret[places[j]].astype(F32) + w_own * suf_out[j]
         out_ref[j] = (num / total).astype(out_ref.dtype)
 
-    for r in far_first(n_own):
-        answer(r).wait_send()
-        answer_stat(r).wait_send()
+    for row in others():
+        answer(row).wait_send()
+        answer_stat(row).wait_send()
 
     @pl.when(is_ring)
     def _():
@@ -365,9 +395,9 @@
 
     @pl.when(is_post)
     def _():
-        for r in far_first(n_own):
-            ask(0, r).wait_send()
-            ask(1, r).wait_send()
+        for row in others():
+            ask(0, row).wait_send()
+            ask(1, row).wait_send()
         hand().wait_send()
 
 
@@ -402,6 +432,7 @@
                 pltpu.VMEM((per_dev, heads, DL), F32),
                 pltpu.VMEM((per_dev, heads, 128), F32),
                 pltpu.VMEM((per_dev, heads, 128), F32),
+                pltpu.VMEM((n_own * heads, 128), jnp.int32),
                 dma((6,)),
                 dma((ring,)),
                 dma((ring,)),

time: 71.6 us -> 68.1 us (0.951)
  Pallas kernels: 70 us -> 65.9 us
    pallas_call x1, Pallas kernels: 70 us -> 65.9 us  [body(): pl.pallas_call(functools.partial(kernel, n_own, n_slice), out_shape=jax.S...]
where the time goes in v4:
time: 68.1 us; the launch traced here: 67.3 us
  Pallas kernels  65.9 us (97%)
  local copies, waits for them, and re-layouts  1.38 us (2%)
    pallas_call x1, Pallas kernels, body(): pl.pallas_call(functools.partial(kernel, n_own, n_slice), out_shape=jax.S...  65.9 us
    unnamed x1, local copies, waits for them, and re-layouts  1.38 us

profile of v4, /device:TPU:65, one launch (start us, length us, event | category | flops | bytes accessed | tf_op | source)
XLA Modules:
  0.0 67.3 jit_solution(2031803508758813143)
XLA Ops:
  0.0 65.9 %shard_map.64 = bf16[4,8,512]{2,1,0:T(8,128)(2,1)} custom-call(s32[512]{0:T(512)} %sp_hbm.1, s32[32]{0:T(128)} %ps_hbm.1, s32[4]{0:T(128)} %sl_hbm.1, bf16[4,8,576]{2,1,0:T(8,128)(2,1)} %q_hbm.1, bf16[2,576,128]{2,1,0:T(8,128)(2,1)} %bitcast.1, bf16[4,64,576]{2,1,0:T(8,128)(2,1)} %suffix_hbm.1), custom_call_target="tpu_custom_call" | custom-call | tf_op jit(solution)/shard_map/pallas_call | solution.py:413
  66.0 1.4 %copy.8 = bf16[4,8,512]{2,1,0:T(8,128)(2,1)} copy(bf16[4,8,512]{2,1,0:T(8,128)(2,1)} %shard_map.64) | data formatting | bytes 65536

commit v5 on v4

--- a/solution.py
+++ b/solution.py
@@ -52,6 +52,9 @@
     suf_top,
     suf_tot,
     parity,
+    part_top,
+    part_tot,
+    part_out,
     local_sem,
     ring_send,
     ring_recv,
@@ -87,7 +90,7 @@
         pltpu.make_async_copy(sl_hbm, sl_ref, local_sem.at[4]),
         pltpu.make_async_copy(suffix_hbm, suf_vm, local_sem.at[5]),
     ]
-    for load in loads:
+    for load in loads[:5]:
         load.start()
 
     barrier = pltpu.get_barrier_semaphore()
@@ -246,49 +249,47 @@
     def others():
         return [lax.rem(z + r, n_own) for r in far_first(n_own)]
 
-    def recent_part():
-        loads[4].wait()
-        loads[5].wait()
-        suf_tokens = suf_vm.shape[1]
-        token = lax.broadcasted_iota(jnp.int32, (heads, suf_tokens), 1)
-        for j in range(per_dev):
-            recent = suf_vm[j]
-            s = lax.dot_general(q_vm[j], recent, NT, preferred_element_type=F32) * scaling
-            s = jnp.where(token < sl_ref[j], s, -1e30)
-            m = jnp.max(s, axis=1, keepdims=True)
-            p = jnp.exp(s - m)
-            suf_top[j] = jnp.broadcast_to(m, (heads, 128))
-            suf_tot[j] = jnp.broadcast_to(jnp.sum(p, axis=1, keepdims=True), (heads, 128))
-            suf_out[j] = jnp.dot(p.astype(BF16), recent[:, :DL], preferred_element_type=F32)
-
-        row_place = lax.broadcasted_iota(jnp.int32, (rows, 128), 0) // heads
-        odds = jnp.zeros((rows, 128), jnp.int32)
+    def recent_part(j):
+        recent = suf_vm[j]
+        token = lax.broadcasted_iota(jnp.int32, (heads, recent.shape[0]), 1)
+        s = lax.dot_general(q_vm[j], recent, NT, preferred_element_type=F32) * scaling
+        s = jnp.where(token < sl_ref[j], s, -1e30)
+        m = jnp.max(s, axis=1, keepdims=True)
+        p = jnp.exp(s - m)
+        suf_top[j] = jnp.broadcast_to(m, (heads, 128))
+        suf_tot[j] = jnp.broadcast_to(jnp.sum(p, axis=1, keepdims=True), (heads, 128))
+        suf_out[j] = jnp.dot(p.astype(BF16), recent[:, :DL], preferred_element_type=F32)
+
+    def parity_part():
+        place = lax.broadcasted_iota(jnp.int32, (heads, 128), 0)
         for row in range(n_own):
             first = (row * n_slice + x) * per_dev
             odd = jnp.int32(0)
             for j in range(per_dev):
                 slot = ps_ref[sp_ref[first + j]]
                 odd = jnp.where((slot >> 1) == z, slot & 1, odd)
-            odds = jnp.where(row_place == row, odd, odds)
-        parity[...] = odds
+            parity[row * heads : (row + 1) * heads, :] = jnp.where(place >= 0, odd, 0)
 
     @pl.when(is_ring)
     def _():
-        loads[1].wait()
         loads[0].wait()
         pl.semaphore_wait(barrier, 3)
-        raw().start()
         for k in range(len(pieces(0, 1))):
             for side in (0, 1):
                 ring(side, 1, pieces(side, 1)[k]).start()
-        loads[2].wait()
-        loads[3].wait()
-        recent_part()
-        for side, d, piece in every_piece():
+        loads[5].start()
+        loads[1].wait()
+        raw().start()
+        for load in loads[2:]:
+            load.wait()
+        filler = [functools.partial(recent_part, j) for j in range(per_dev)] + [parity_part]
+        for k, (side, d, piece) in enumerate(every_piece()):
             ring(side, d, piece).wait_recv()
             if d < last and piece in pieces(side, d + 1):
                 ring(side, d + 1, piece).start()
             pair(side, d, piece).start()
+            if k % 2 == 1 and filler:
+                filler.pop(0)()
 
     @pl.when(is_post)
     def _():
@@ -304,7 +305,7 @@
 
         for row in range(n_own):
             stage[0, row] = q_vm[sample_of(row)]
-        recent_part()
+        loads[5].start()
         raw().wait_recv()
         for row in range(n_own):
             stage[1, row] = q_pair[sample_of(row)]
@@ -314,30 +315,41 @@
             ask(0, row).start()
             ask(1, row).start()
         hand().start()
+        loads[4].wait()
+        loads[5].wait()
+        parity_part()
+        for j in range(per_dev):
+            recent_part(j)
         for side, d, piece in every_piece():
-            pair(side, d, piece).wait_recv()
-
-    def attend(lo, hi):
+            if d < last:
+                pair(side, d, piece).wait_recv()
+
+    def collect(lo, hi):
         for row in range(lo, hi):
 
             @pl.when(jnp.logical_or(is_ring, z != row))
             def _():
                 asked_by(row).wait_recv()
 
+    def weigh(lo, hi, begin, end):
         size = (hi - lo) * heads
         is_odd = parity[lo * heads : hi * heads, :1] > 0
         q = arrived[lo:hi].reshape(size, feat)
-        s0 = jnp.dot(q, keys[0], preferred_element_type=F32)
-        s1 = jnp.dot(q, keys[1], preferred_element_type=F32)
+        s0 = jnp.dot(q, keys[0, :, begin:end], preferred_element_type=F32)
+        s1 = jnp.dot(q, keys[1, :, begin:end], preferred_element_type=F32)
         s = jnp.where(is_odd, s1, s0) * scaling
         m = jnp.max(s, axis=1, keepdims=True)
         p = jnp.exp(s - m)
         l = jnp.sum(p, axis=1, keepdims=True)
+        even = jnp.where(is_odd, 0.0, p).astype(BF16)
+        odd = jnp.where(is_odd, p, 0.0).astype(BF16)
         out = lax.dot_general(
-            jnp.where(is_odd, 0.0, p).astype(BF16), keys[0, :DL], NT, preferred_element_type=F32
-        ) + lax.dot_general(
-            jnp.where(is_odd, p, 0.0).astype(BF16), keys[1, :DL], NT, preferred_element_type=F32
-        )
+            even, keys[0, :DL, begin:end], NT, preferred_element_type=F32
+        ) + lax.dot_general(odd, keys[1, :DL, begin:end], NT, preferred_element_type=F32)
+        return m, l, out
+
+    def give(lo, hi, m, l, out):
+        size = (hi - lo) * heads
         lane = lax.broadcasted_iota(jnp.int32, (size, 128), 1)
         sub = lax.rem(lax.broadcasted_iota(jnp.int32, (size, 128), 0), heads)
         both = jnp.where(lane == sub, m, 0.0) + jnp.where(lane == sub + heads, l, 0.0)
@@ -353,11 +365,48 @@
                 answer(row).start()
                 answer_stat(row).start()
 
-    cuts = [0, n_own // SHARE, n_own]
-    for lo, hi in zip(cuts, cuts[1:]):
-        attend(lo, hi)
+    cut = n_own // SHARE
+    near = (n_slice - 1) * tok
+    collect(0, cut)
+    m0, l0, out0 = weigh(0, cut, 0, near)
+    part_top[...] = jnp.broadcast_to(m0, (cut * heads, 128))
+    part_tot[...] = jnp.broadcast_to(l0, (cut * heads, 128))
+    part_out[...] = out0
+
+    @pl.when(is_post)
+    def _():
+        for side, d, piece in every_piece():
+            if d == last:
+                pair(side, d, piece).wait_recv()
+
+    m1, l1, out1 = weigh(0, cut, near, near + tok)
+    m0 = part_top[:, :1]
+    m = jnp.maximum(m0, m1)
+    fade0 = jnp.exp(m0 - m)
+    fade1 = jnp.exp(m1 - m)
+    give(0, cut, m, part_tot[:, :1] * fade0 + l1 * fade1, part_out[...] * fade0 + out1 * fade1)
+    collect(cut, n_own)
+    give(cut, n_own, *weigh(cut, n_own, 0, n_slice * tok))
     ret[z] = res[z]
     ret_stat[z] = stat[z]
+
+    for row in others():
+        answer(row).wait_send()
+        answer_stat(row).wait_send()
+
+    @pl.when(is_ring)
+    def _():
+        raw().wait_send()
+        for side, d, piece in every_piece():
+            ring(side, d, piece).wait_send()
+            pair(side, d, piece).wait_send()
+
+    @pl.when(is_post)
+    def _():
+        for row in others():
+            ask(0, row).wait_send()
+            ask(1, row).wait_send()
+        hand().wait_send()
 
     places = own_places()
     for row in range(n_own):
@@ -381,24 +430,6 @@
         total = w_pre * pre_tot + w_own * own_tot
         num = w_pre * ret[places[j]].astype(F32) + w_own * suf_out[j]
         out_ref[j] = (num / total).astype(out_ref.dtype)
-
-    for row in others():
-        answer(row).wait_send()
-        answer_stat(row).wait_send()
-
-    @pl.when(is_ring)
-    def _():
-        raw().wait_send()
-        for side, d, piece in every_piece():
-            ring(side, d, piece).wait_send()
-            pair(side, d, piece).wait_send()
-
-    @pl.when(is_post)
-    def _():
-        for row in others():
-            ask(0, row).wait_send()
-            ask(1, row).wait_send()
-        hand().wait_send()
 
 
 def solution(mesh):
@@ -433,6 +464,9 @@
                 pltpu.VMEM((per_dev, heads, 128), F32),
                 pltpu.VMEM((per_dev, heads, 128), F32),
                 pltpu.VMEM((n_own * heads, 128), jnp.int32),
+                pltpu.VMEM((n_own // SHARE * heads, 128), F32),
+                pltpu.VMEM((n_own // SHARE * heads, 128), F32),
+                pltpu.VMEM((n_own // SHARE * heads, DL), F32),
                 dma((6,)),
                 dma((ring,)),
                 dma((ring,)),

time: 68.1 us -> 67.9 us (level)
  no operation moved by 1% of the time
where the time goes in v5:
time: 67.9 us; the launch traced here: 67.7 us
  Pallas kernels  66.3 us (98%)
  local copies, waits for them, and re-layouts  1.38 us (2%)
    pallas_call x1, Pallas kernels, body(): pl.pallas_call(functools.partial(kernel, n_own, n_slice), out_shape=jax.S...  66.3 us
    unnamed x1, local copies, waits for them, and re-layouts  1.38 us

profile of v5, /device:TPU:65, one launch (start us, length us, event | category | flops | bytes accessed | tf_op | source)
XLA Modules:
  0.0 67.7 jit_solution(6712732982763652097)
XLA Ops:
  0.0 66.3 %shard_map.64 = bf16[4,8,512]{2,1,0:T(8,128)(2,1)} custom-call(s32[512]{0:T(512)} %sp_hbm.1, s32[32]{0:T(128)} %ps_hbm.1, s32[4]{0:T(128)} %sl_hbm.1, bf16[4,8,576]{2,1,0:T(8,128)(2,1)} %q_hbm.1, bf16[2,576,128]{2,1,0:T(8,128)(2,1)} %bitcast.1, bf16[4,64,576]{2,1,0:T(8,128)(2,1)} %suffix_hbm.1), custom_call_target="tpu_custom_call" | custom-call | tf_op jit(solution)/shard_map/pallas_call | solution.py:444
  66.3 1.4 %copy.8 = bf16[4,8,512]{2,1,0:T(8,128)(2,1)} copy(bf16[4,8,512]{2,1,0:T(8,128)(2,1)} %shard_map.64) | data formatting | bytes 65536

commit v6 on v5

--- a/solution.py
+++ b/solution.py
@@ -90,7 +90,7 @@
         pltpu.make_async_copy(sl_hbm, sl_ref, local_sem.at[4]),
         pltpu.make_async_copy(suffix_hbm, suf_vm, local_sem.at[5]),
     ]
-    for load in loads[:5]:
+    for load in loads:
         load.start()
 
     barrier = pltpu.get_barrier_semaphore()
@@ -277,7 +277,6 @@
         for k in range(len(pieces(0, 1))):
             for side in (0, 1):
                 ring(side, 1, pieces(side, 1)[k]).start()
-        loads[5].start()
         loads[1].wait()
         raw().start()
         for load in loads[2:]:
@@ -305,7 +304,6 @@
 
         for row in range(n_own):
             stage[0, row] = q_vm[sample_of(row)]
-        loads[5].start()
         raw().wait_recv()
         for row in range(n_own):
             stage[1, row] = q_pair[sample_of(row)]

time: 67.9 us -> 67.9 us (level)
  no operation moved by 1% of the time
where the time goes in v6:
time: 67.9 us; the launch traced here: 67.7 us
  Pallas kernels  66.3 us (98%)
  local copies, waits for them, and re-layouts  1.38 us (2%)
    pallas_call x1, Pallas kernels, body(): pl.pallas_call(functools.partial(kernel, n_own, n_slice), out_shape=jax.S...  66.3 us
    unnamed x1, local copies, waits for them, and re-layouts  1.38 us

profile of v6, /device:TPU:65, one launch (start us, length us, event | category | flops | bytes accessed | tf_op | source)
XLA Modules:
  0.0 67.7 jit_solution(14777058082856274624)
XLA Ops:
  0.0 66.3 %shard_map.64 = bf16[4,8,512]{2,1,0:T(8,128)(2,1)} custom-call(s32[512]{0:T(512)} %sp_hbm.1, s32[32]{0:T(128)} %ps_hbm.1, s32[4]{0:T(128)} %sl_hbm.1, bf16[4,8,576]{2,1,0:T(8,128)(2,1)} %q_hbm.1, bf16[2,576,128]{2,1,0:T(8,128)(2,1)} %bitcast.1, bf16[4,64,576]{2,1,0:T(8,128)(2,1)} %suffix_hbm.1), custom_call_target="tpu_custom_call" | custom-call | tf_op jit(solution)/shard_map/pallas_call | solution.py:442
  66.3 1.4 %copy.8 = bf16[4,8,512]{2,1,0:T(8,128)(2,1)} copy(bf16[4,8,512]{2,1,0:T(8,128)(2,1)} %shard_map.64) | data formatting | bytes 65536
